TPU v7x, 128 devices: a whole 4x4x4 slice. The times are simulated.
128 devices in a mesh: row: 4 (over x), col: 4 (over y_lo, core), layer: 8 (over y_hi, z).
Axes of the slice: x: 4, y: 4 (y_hi: 2, y_lo: 2; y = y_hi * 2 + y_lo), z: 4, core: 2. Of those that a mesh axis runs over, the one named last changes fastest.
Arguments:
- left_factor: float32 [6144, 8192], P('row', 'col'), may hold values from -6 to 6
- right_factor: float32 [8192, 6144], P('row', 'col'), may hold values from -0.0625 to 0.0625
Outputs:
- product: float32 [6144, 6144], P(('row', 'layer'), 'col')
All inputs are finite; a program needn't handle non-finite values.
Results may differ from a plain program's by a relative error of at most 0.000073.
Values sent between devices are 32-bit elements; how exact they have to be, the bound alone decides.
A program may use at most 192 MiB of HBM per device.

v0:
```python
import jax
import jax.numpy as jnp
from jax import lax
from jax.sharding import PartitionSpec as P

K = 8192
STEPS = 2


def broadcast(value, axis, root):
    mine = lax.axis_index(axis) == root
    return lax.psum(jnp.where(mine, value, jnp.zeros_like(value)), axis)


def per_device(left_factor, right_factor):
    block_depth = left_factor.shape[1]
    layers = lax.axis_size("layer")
    depth_index = lax.axis_index("layer")
    panel_width = K // (layers * STEPS)
    per_block = block_depth // panel_width
    group_size = 1
    gathered = []
    for step_index in range(0, STEPS, group_size):
        first_panel = depth_index * STEPS + step_index
        source = first_panel // per_block
        offset = first_panel % per_block * panel_width
        left_piece = lax.dynamic_slice_in_dim(left_factor, offset, group_size * panel_width, 1)
        right_piece = lax.dynamic_slice_in_dim(right_factor, offset, group_size * panel_width, 0)
        fetch_left_panel = broadcast(left_piece, "col", source)
        fetch_right_panel = broadcast(right_piece, "row", source)
        gathered.append((fetch_left_panel, fetch_right_panel))
    total = jnp.zeros((left_factor.shape[0], right_factor.shape[1]), jnp.float32)
    for left_panel, right_panel in gathered:
        total = total + jnp.dot(
            left_panel,
            right_panel,
            precision=lax.Precision.HIGHEST,
            preferred_element_type=jnp.float32,
        )
    return lax.psum_scatter(total, "layer", scatter_dimension=0, tiled=True)


def solution(mesh):
    placed = (P("row", "col"), P("row", "col"))
    return jax.shard_map(
        per_device,
        mesh=mesh,
        in_specs=placed,
        out_specs=P(("row", "layer"), "col"),
        check_vma=False,
    )
```

profile of v0, /device:TPU:0, one launch (start us, length us, event | category | flops | bytes accessed | tf_op | source)
XLA Modules:
  0.0 438.1 jit_solution(5593754253861912896)
XLA Ops:
  6.5 0.0 all-reduce.5.cloned.1.call-start
  6.5 6.3 %dynamic-slice_select_fusion.1 = (f32[1536,512]{1,0:T(8,128)}, f32[1536,512]{1,0:T(8,128)}) fusion(f32[1536,2048]{1,0:T(8,128)} %param.2, s32[]{:T(128)S(6)} %select_n.64, pred[]{:T(512)S(6)} %eq.17, s32[]{:T(128)S(6)} %select_n.57, pred[]{:T(512)S(6)} %eq.15), kind=kLoop, calls=%fused_computation.2 | loop fusion | flops 1572864 | bytes 12582922 | tf_op jit(solution)/shard_map/jit(_where)/select_n | solution.py:12
  12.8 0.0 all-reduce.5.cloned.1.call-update
  12.9 0.0 all-reduce.7.cloned.1.call-start
  12.9 6.1 %dynamic-slice_select_fusion = (f32[512,1536]{1,0:T(8,128)}, f32[512,1536]{1,0:T(8,128)}) fusion(f32[2048,1536]{1,0:T(8,128)} %param.3, s32[]{:T(128)S(6)} %select_n.64, pred[]{:T(512)S(6)} %eq.18, s32[]{:T(128)S(6)} %select_n.57, pred[]{:T(512)S(6)} %eq.16), kind=kLoop, calls=%fused_computation.1 | loop fusion | flops 1572864 | bytes 12582922 | tf_op jit(solution)/shard_map/jit(_where)/select_n | solution.py:12
  19.0 0.0 all-reduce.7.cloned.1.call-update
  19.1 0.0 reduce-scatter.2.cloned.1.call-start
  19.1 121.6 %all-reduce.5.cloned.1.call-done = (f32[1536,512]{1,0:T(8,128)}, f32[1536,512]{1,0:T(8,128)}) async-done(((f32[1536,512]{1,0:T(8,128)}, f32[1536,512]{1,0:T(8,128)}), (f32[1536,512]{1,0:T(8,128)}, f32[1536,512]{1,0:T(8,128)})) %all-reduce.5.cloned.1.call-update) | async-done | bytes 6291472 | tf_op jit(solution)/shard_map/psum | solution.py:12
  140.7 130.3 %all-reduce.7.cloned.1.call-done = (f32[512,1536]{1,0:T(8,128)}, f32[512,1536]{1,0:T(8,128)}) async-done(((f32[512,1536]{1,0:T(8,128)}, f32[512,1536]{1,0:T(8,128)}), (f32[512,1536]{1,0:T(8,128)}, f32[512,1536]{1,0:T(8,128)})) %all-reduce.7.cloned.1.call-update) | async-done | bytes 6291472 | tf_op jit(solution)/shard_map/psum | solution.py:12
  271.1 0.0 copy-start
  271.1 0.0 copy-start.1
  271.1 19.7 %fusion = f32[1536,1536]{1,0:T(8,128)S(1)} fusion(f32[1536,512]{1,0:T(8,128)} %get-tuple-element.5, f32[512,1536]{1,0:T(8,128)} %get-tuple-element.7), kind=kOutput, calls=%fused_computation.5 | convolution fusion | flops 14495514624 | bytes 15728640 | tf_op jit(solution)/shard_map/dot_general | solution.py:34
  290.8 0.0 copy-done
  290.8 0.0 copy-done.1
  290.8 18.6 %convolution_add_fusion = f32[1536,1536]{1,0:T(8,128)} fusion(f32[1536,1536]{1,0:T(8,128)S(1)} %fusion, f32[1536,512]{1,0:T(8,128)S(1)} %copy-done, f32[512,1536]{1,0:T(8,128)S(1)} %copy-done.1), kind=kOutput, calls=%fused_computation | convolution fusion | flops 14497873920 | bytes 25165824 | tf_op jit(solution)/shard_map/dot_general | solution.py:34
  309.3 0.0 reduce-scatter.2.cloned.1.call-update
  309.3 122.3 %reduce-scatter.2.cloned.1.call-done = f32[192,1536]{1,0:T(8,128)} async-done(((f32[1536,1536]{1,0:T(8,128)}), f32[192,1536]{1,0:T(8,128)}) %reduce-scatter.2.cloned.1.call-update) | async-done | bytes 1179664 | tf_op jit(solution)/shard_map/reduce_scatter | solution.py:40
Async XLA Ops:
  6.5 134.2 %all-reduce.5.cloned.1.call-start = ((), (), s32[]{:S(2)}) async-start(), calls=%async_computation.2 | async-start | bytes 12582912 | tf_op jit(solution)/shard_map/psum | solution.py:12
  12.9 258.2 %all-reduce.7.cloned.1.call-start = ((), (), s32[]{:S(2)}) async-start(), calls=%async_computation.3 | async-start | bytes 12582912 | tf_op jit(solution)/shard_map/psum | solution.py:12
  19.1 412.5 %reduce-scatter.2.cloned.1.call-start = ((), (), s32[]{:S(2)}) async-start(), calls=%async_computation.1 | async-start | bytes 10616832 | tf_op jit(solution)/shard_map/reduce_scatter | solution.py:40
  271.1 19.7 %copy-start = (f32[1536,512]{1,0:T(8,128)S(1)}, f32[1536,512]{1,0:T(8,128)}, u32[]{:S(2)}) copy-start(f32[1536,512]{1,0:T(8,128)} %get-tuple-element.6) | copy-start | bytes 9437188
  271.1 19.7 %copy-start.1 = (f32[512,1536]{1,0:T(8,128)S(1)}, f32[512,1536]{1,0:T(8,128)}, u32[]{:S(2)}) copy-start(f32[512,1536]{1,0:T(8,128)} %get-tuple-element.8) | copy-start | bytes 9437188
Sparse Core Ops, SparseCore 0:
  13.0 127.6 all-reduce.4
  143.1 127.9 all-reduce.6
  309.5 122.1 reduce-scatter.1
where the time goes:
time: 438 us
  waiting for transfers between devices  374 us (85%)
  matrix products  38.2 us (9%)
  between operations  13.1 us (3%)
  other arithmetic  12.4 us (3%)
    psum x2, waiting for transfers between devices, broadcast(): return lax.psum(jnp.where(mine, value, jnp.zeros_like(value)), axis)  252 us
    reduce_scatter x1, waiting for transfers between devices, per_device(): return lax.psum_scatter(total, 'layer', scatter_dimension=0, tiled=True)  122 us
    dot_general x2, matrix products, per_device(): jnp.dot(left_panel, right_panel, precision=lax.Precision.HIGHEST, preferr...  38.2 us
    select_n x2, other arithmetic, broadcast(): return lax.psum(jnp.where(mine, value, jnp.zeros_like(value)), axis)  12.4 us
  transfers between devices with their start and end apart: 3, of which 3 were waited for; matrix products, arithmetic and copies ran while one was open for 1% of the time, Pallas kernels for 0%

commit v1 on v0

--- a/solution.py
+++ b/solution.py
@@ -9,7 +9,7 @@
 
 def broadcast(value, axis, root):
     mine = lax.axis_index(axis) == root
-    return lax.psum(jnp.where(mine, value, jnp.zeros_like(value)), axis)
+    return jnp.sum(lax.all_gather(jnp.where(mine, value, jnp.zeros_like(value)), axis), axis=0)
 
 
 def per_device(left_factor, right_factor):

time: 438 us -> 669 us (1.53)
  waiting for transfers between devices: 374 us -> 574 us
  other arithmetic: 12.4 us -> 42.9 us
    all_gather x0 -> x4, waiting for transfers between devices: none -> 450 us  [broadcast(): lax.all_gather(jnp.where(mine, value, jnp.zeros_like(value)), axis)]
    psum x2 -> x0, waiting for transfers between devices: 252 us -> none  [broadcast(): return lax.psum(jnp.where(mine, value, jnp.zeros_like(value)), axis)]
    reduce_sum x0 -> x4, other arithmetic: none -> 30.6 us  [broadcast(): jnp.sum(lax.all_gather(jnp.where(mine, value, jnp.zeros_like(value)), axi...]
  transfers between devices with their start and end apart: 3 -> 5, of which waited for: 3 -> 5; matrix products, arithmetic and copies ran while one was open for 1% -> 4% of each run, Pallas kernels for 0% -> 0%
where the time goes in v1:
time: 669 us
  waiting for transfers between devices  574 us (86%)
  other arithmetic  42.9 us (6%)
  matrix products  38.4 us (6%)
  between operations  13.2 us (2%)
    all_gather x4, waiting for transfers between devices, broadcast(): lax.all_gather(jnp.where(mine, value, jnp.zeros_like(value)), axis)  450 us
    reduce_scatter x1, waiting for transfers between devices, per_device(): return lax.psum_scatter(total, 'layer', scatter_dimension=0, tiled=True)  123 us
    dot_general x2, matrix products, per_device(): jnp.dot(left_panel, right_panel, precision=lax.Precision.HIGHEST, preferr...  38.4 us
    reduce_sum x4, other arithmetic, broadcast(): jnp.sum(lax.all_gather(jnp.where(mine, value, jnp.zeros_like(value)), axi...  30.6 us
  transfers between devices with their start and end apart: 5, of which 5 were waited for; matrix products, arithmetic and copies ran while one was open for 4% of the time, Pallas kernels for 0%

profile of v1, /device:TPU:0, one launch (start us, length us, event | category | flops | bytes accessed | tf_op | source)
XLA Modules:
  0.0 668.8 jit_solution(249793192000669475)
XLA Ops:
  6.5 0.0 all-gather.13.cloned.1.call-start
  6.5 6.2 dynamic-slice_select_fusion.1
  12.7 0.0 all-gather.13.cloned.1.call-update
  12.8 0.0 all-gather.9.cloned.1.call-start
  12.8 0.7 all-gather.9.cloned.1.call-update
  13.5 0.0 all-gather.15.cloned.1.call-start
  13.6 6.1 dynamic-slice_select_fusion
  19.7 0.0 all-gather.15.cloned.1.call-update
  19.7 0.0 all-gather.11.cloned.1.call-start
  19.7 0.5 all-gather.11.cloned.1.call-update
  20.3 0.0 reduce-scatter.2.cloned.1.call-start
  20.3 109.4 %all-gather.13.cloned.1.call-done = f32[6144,512]{1,0:T(8,128)} async-done(((f32[1536,512]{1,0:T(8,128)}), f32[6144,512]{1,0:T(8,128)}) %all-gather.13.cloned.1.call-update) | async-done | bytes 12582928 | tf_op jit(solution)/shard_map/all_gather | solution.py:12
  129.7 6.5 reduce_sum.38
  136.2 112.3 %all-gather.9.cloned.1.call-done = f32[6144,512]{1,0:T(8,128)} async-done(((f32[1536,512]{1,0:T(8,128)}), f32[6144,512]{1,0:T(8,128)}) %all-gather.9.cloned.1.call-update) | async-done | bytes 12582928 | tf_op jit(solution)/shard_map/all_gather | solution.py:12
  248.5 8.1 %reduce_sum.36 = f32[1536,512]{1,0:T(8,128)} reduce(f32[4,1536,512]{2,1,0:T(8,128)} %bitcast.9, f32[]{:T(128)} %constant.58.clone.1), dimensions={0}, to_apply=%region_0.1 | reduce | flops 2359296 | bytes 15728644 | tf_op jit(solution)/shard_map/reduce_sum | solution.py:12
  256.7 114.9 %all-gather.15.cloned.1.call-done = f32[2048,1536]{1,0:T(8,128)} async-done(((f32[512,1536]{1,0:T(8,128)}), f32[2048,1536]{1,0:T(8,128)}) %all-gather.15.cloned.1.call-update) | async-done | bytes 12582928 | tf_op jit(solution)/shard_map/all_gather | solution.py:12
  371.5 8.0 %reduce_sum.39 = f32[512,1536]{1,0:T(8,128)} reduce(f32[4,512,1536]{2,1,0:T(8,128)} %bitcast.10, f32[]{:T(128)} %constant.58.clone.1), dimensions={0}, to_apply=%region_3.4 | reduce | flops 2359296 | bytes 15728644 | tf_op jit(solution)/shard_map/reduce_sum | solution.py:12
  379.5 113.1 %all-gather.11.cloned.1.call-done = f32[2048,1536]{1,0:T(8,128)} async-done(((f32[512,1536]{1,0:T(8,128)}), f32[2048,1536]{1,0:T(8,128)}) %all-gather.11.cloned.1.call-update) | async-done | bytes 12582928 | tf_op jit(solution)/shard_map/all_gather | solution.py:12
  492.6 8.0 %reduce_sum.37 = f32[512,1536]{1,0:T(8,128)} reduce(f32[4,512,1536]{2,1,0:T(8,128)} %bitcast.11, f32[]{:T(128)} %constant.58.clone.1), dimensions={0}, to_apply=%region_1.2 | reduce | flops 2359296 | bytes 15728644 | tf_op jit(solution)/shard_map/reduce_sum | solution.py:12
  500.6 0.0 copy-start
  500.6 19.7 %fusion = f32[1536,1536]{1,0:T(8,128)S(1)} fusion(f32[1536,512]{1,0:T(8,128)} %reduce_sum.36, f32[512,1536]{1,0:T(8,128)} %reduce_sum.37), kind=kOutput, calls=%fused_computation.5 | convolution fusion | flops 14495514624 | bytes 15728640 | tf_op jit(solution)/shard_map/dot_general | solution.py:34
  520.3 0.0 copy-done
  520.3 18.7 %convolution_add_fusion = f32[1536,1536]{1,0:T(8,128)} fusion(f32[1536,1536]{1,0:T(8,128)S(1)} %fusion, f32[1536,512]{1,0:T(8,128)S(1)} %reduce_sum.38, f32[512,1536]{1,0:T(8,128)S(1)} %copy-done), kind=kOutput, calls=%fused_computation | convolution fusion | flops 14497873920 | bytes 25165824 | tf_op jit(solution)/shard_map/dot_general | solution.py:34
  539.0 0.0 reduce-scatter.2.cloned.1.call-update
  539.0 123.2 %reduce-scatter.2.cloned.1.call-done = f32[192,1536]{1,0:T(8,128)} async-done(((f32[1536,1536]{1,0:T(8,128)}), f32[192,1536]{1,0:T(8,128)}) %reduce-scatter.2.cloned.1.call-update) | async-done | bytes 1179664 | tf_op jit(solution)/shard_map/reduce_scatter | solution.py:40
Async XLA Ops:
  6.5 123.2 %all-gather.13.cloned.1.call-start = ((), (), s32[]{:S(2)}) async-start(), calls=%async_computation.4 | async-start | bytes 15728640 | tf_op jit(solution)/shard_map/all_gather | solution.py:12
  12.8 235.8 %all-gather.9.cloned.1.call-start = ((), (), s32[]{:S(2)}) async-start(), calls=%async_computation.2 | async-start | bytes 15728640 | tf_op jit(solution)/shard_map/all_gather | solution.py:12
  13.5 358.0 %all-gather.15.cloned.1.call-start = ((), (), s32[]{:S(2)}) async-start(), calls=%async_computation.5 | async-start | bytes 15728640 | tf_op jit(solution)/shard_map/all_gather | solution.py:12
  19.7 472.9 %all-gather.11.cloned.1.call-start = ((), (), s32[]{:S(2)}) async-start(), calls=%async_computation.3 | async-start | bytes 15728640 | tf_op jit(solution)/shard_map/all_gather | solution.py:12
  20.3 642.0 %reduce-scatter.2.cloned.1.call-start = ((), (), s32[]{:S(2)}) async-start(), calls=%async_computation.1 | async-start | bytes 10616832 | tf_op jit(solution)/shard_map/reduce_scatter | solution.py:40
  500.6 19.7 %copy-start = (f32[512,1536]{1,0:T(8,128)S(1)}, f32[512,1536]{1,0:T(8,128)}, u32[]{:S(2)}) copy-start(f32[512,1536]{1,0:T(8,128)} %reduce_sum.39) | copy-start | bytes 9437188
Sparse Core Ops, SparseCore 0:
  12.9 116.7 all-gather.12
  131.4 117.1 all-gather.8
  250.2 121.3 all-gather.14
  373.0 119.4 all-gather.10
  539.2 123.0 reduce-scatter.1
